TPU v7x, 32 devices: a whole 2x2x4 slice. The times are simulated.
32 devices in a mesh: kvp: 16 (over z, y, x), tp: 2 (over core).
Axes of the slice: x: 2, y: 2, z: 4, core: 2. Of those that a mesh axis runs over, the one named last changes fastest.
Arguments:
- queries: bfloat16 [8, 8192], P(None, 'tp'), may hold values from -12 to 12
- key_pool: bfloat16 [512, 64, 1024], P('kvp', None, 'tp'), may hold values from -5 to 5
- value_pool: bfloat16 [512, 64, 1024], P('kvp', None, 'tp'), may hold values from -5 to 5
- block_table: int32 [16, 32], P('kvp'), may hold values from 0 to 31, each once within a row
- lengths: int32 [8], replicated, may hold values from 1 to 4096, 20480 in all
- residual_in: float32 [8, 8192], P(None, 'kvp'), may hold values from -12 to 12
- out_weight: bfloat16 [8192, 8192], P('tp', 'kvp'), may hold values from -0.0625 to 0.0625
- norm_gain: bfloat16 [8192], P('kvp'), may hold values from 0.25 to 1.75
- gate_weight: bfloat16 [8192, 28672], P('kvp', 'tp'), may hold values from -0.0625 to 0.0625
- up_weight: bfloat16 [8192, 28672], P('kvp', 'tp'), may hold values from -0.0625 to 0.0625
- down_weight: bfloat16 [28672, 8192], P('tp', 'kvp'), may hold values from -0.03125 to 0.03125
Outputs:
- attended: bfloat16 [8, 8192], P(None, 'tp')
- layer_out: float32 [8, 8192], P(None, 'kvp')
Inputs may be any that keep to these rules, and one draw needn't show every extreme that they name: Row s is a permutation of 0 to 31; the page of request b's block j in KV shard s is s * 32 + block_table[s, b * 4 + j]. The lengths sum to 20480 and the longest is exactly 4096.
All inputs are finite; a program needn't handle non-finite values.
Results may differ from a plain program's by a relative error of at most 0.0056.
Values may be sent and summed in bfloat16 or wider, within the bound.
A program may use at most 128 MiB of HBM per device.

v0:
```python
import jax
import jax.numpy as jnp
from jax import lax
from jax.sharding import PartitionSpec as P

D = 8192
HD = 128


def merged(part, axis, combine):
    gathered = jax.tree.map(lambda a: lax.all_gather(a, axis), part)

    def take(source):
        return jax.tree.map(lambda a: lax.dynamic_index_in_dim(a, source, 0, False), gathered)

    return lax.fori_loop(
        1, lax.axis_size(axis), lambda source, state: combine(state, take(source)), take(0)
    )


def combine(earlier, later):
    peak_early, sum_early, out_early = earlier
    peak_late, sum_late, out_late = later
    row_peak = jnp.maximum(peak_early, peak_late)
    factor_early = jnp.exp(peak_early - row_peak)
    factor_late = jnp.exp(peak_late - row_peak)
    weight_sum = sum_early * factor_early + sum_late * factor_late
    out_sum = out_early * factor_early[..., None] + out_late * factor_late[..., None]
    return (row_peak, weight_sum, out_sum)


def body(
    queries,
    key_pool,
    value_pool,
    block_table,
    lengths,
    residual_in,
    out_weight,
    norm_gain,
    gate_weight,
    up_weight,
    down_weight,
):
    requests = queries.shape[0]
    kv_local = key_pool.shape[2] // HD
    heads_local = queries.shape[1] // HD
    group_size = heads_local // kv_local
    blocks = block_table.shape[1] // requests
    shard_span = blocks * key_pool.shape[1]
    shard_index = lax.axis_index("kvp")
    page_ids = block_table[0].reshape(requests, blocks)
    key_rows = key_pool[page_ids].reshape(requests, shard_span, kv_local, HD)
    value_rows = value_pool[page_ids].reshape(requests, shard_span, kv_local, HD)
    query_heads = queries.reshape(requests, kv_local, group_size, HD)
    scores = jnp.einsum(
        "bkgd,btkd->bkgt", query_heads, key_rows, preferred_element_type=jnp.float32
    ) * HD ** (-0.5)
    positions = shard_index * shard_span + jnp.arange(shard_span, dtype=jnp.int32)
    is_live = (positions[None, :] < lengths[:, None])[:, None, None, :]
    masked = jnp.where(is_live, scores, -1e30)
    row_peak = jnp.max(masked, axis=-1)
    weights = jnp.where(is_live, jnp.exp(masked - row_peak[..., None]), 0.0)
    weight_sum = jnp.sum(weights, axis=-1).reshape(requests, heads_local)
    rounded = weights.astype(jnp.bfloat16)
    out_sum = jnp.einsum("bkgt,btkd->bkgd", rounded, value_rows, preferred_element_type=jnp.float32)
    out_sum = out_sum.reshape(requests, heads_local, HD)
    row_peak = row_peak.reshape(requests, heads_local)
    row_peak, weight_sum, out_sum = merged((row_peak, weight_sum, out_sum), "kvp", combine)
    attended = (
        (out_sum / weight_sum[..., None]).astype(jnp.bfloat16).reshape(requests, heads_local * HD)
    )
    projected = jnp.dot(attended, out_weight, preferred_element_type=jnp.float32)
    mixed = residual_in + lax.psum(projected, "tp")
    squares = lax.psum(jnp.sum(mixed * mixed, axis=1), "kvp")
    inv_rms = lax.rsqrt(squares / D + 0.1)
    normed = (mixed * inv_rms[:, None] * norm_gain.astype(jnp.float32)).astype(jnp.bfloat16)
    gate_part = jnp.dot(normed, gate_weight, preferred_element_type=jnp.float32)
    up_part = jnp.dot(normed, up_weight, preferred_element_type=jnp.float32)
    gate_full, up_full = lax.psum((gate_part, up_part), "kvp")
    hidden = (jax.nn.silu(gate_full) * up_full).astype(jnp.bfloat16)
    down_part = jnp.dot(hidden, down_weight, preferred_element_type=jnp.float32)
    layer_out = mixed + lax.psum(down_part, "tp")
    return (attended, layer_out)


def solution(mesh):
    return jax.shard_map(
        body,
        mesh=mesh,
        in_specs=(
            P(None, "tp"),
            P("kvp", None, "tp"),
            P("kvp", None, "tp"),
            P("kvp", None),
            P(),
            P(None, "kvp"),
            P("tp", "kvp"),
            P("kvp"),
            P("kvp", "tp"),
            P("kvp", "tp"),
            P("tp", "kvp"),
        ),
        out_specs=(P(None, "tp"), P(None, "kvp")),
        check_vma=False,
    )
```

profile of v0, /device:TPU:0, one launch (start us, length us, event | category | flops | bytes accessed | tf_op | source)
XLA Modules:
  0.0 310.6 jit_solution(2432256013141088473)
XLA Ops:
  7.2 0.0 copy-start
  7.2 0.0 all-gather.2.cloned.1.call-start
  7.2 0.5 broadcast.76
  7.8 1.4 reduce.3
  9.1 0.1 reshape_squeeze.3
  9.2 0.1 reshape.83
  9.3 0.0 copy-done
  9.3 2.0 gather_fusion
  11.3 4.0 %reshape.77 = bf16[8,256,4,128]{3,2,1,0:T(4,128)(2,1)} reshape(bf16[32,64,512]{2,1,0:T(8,128)(2,1)} %gather_fusion) | data formatting | bytes 4194304 | tf_op jit(solution)/shard_map/reshape | solution.py:53
  15.3 3.6 %gather_fusion.1 = bf16[32,64,512]{2,1,0:T(8,128)(2,1)} fusion(bf16[32,64,512]{2,1,0:T(8,128)(2,1)} %param.15, s32[1024]{0:T(1024)S(1)} %pad_clamp_fusion), kind=kCustom, calls=%fused_computation.1 | custom fusion | bytes 4194432 | tf_op jit(solution)/shard_map/gather | solution.py:54
  18.9 0.0 copy-start.5
  18.9 0.0 copy-start.6
  18.9 4.0 %reshape.79 = bf16[8,256,4,128]{3,2,1,0:T(4,128)(2,1)} reshape(bf16[32,64,512]{2,1,0:T(8,128)(2,1)} %gather_fusion.1) | data formatting | bytes 4194304 | tf_op jit(solution)/shard_map/reshape | solution.py:54
  22.9 0.0 copy-done.5
  22.9 0.0 copy-start.1
  22.9 0.1 broadcast_compare_fusion
  22.9 0.0 copy-done.6
  23.0 2.5 fusion.34
  25.4 0.0 copy-start.4
  25.4 0.0 copy-done.1
  25.4 1.1 fusion.16
  26.5 0.0 all-gather.2.cloned.1.call-update
  26.6 0.0 all-reduce.3.cloned.1.call-start
  26.6 0.1 all_gather_reshape.9
  26.7 0.2 fusion.22
  26.9 0.1 all_gather_reshape.10
  27.0 0.0 copy-done.4
  27.0 42.8 %all_gather.10 = f32[16,8,32]{2,1,0:T(8,128)S(1)} all-gather(f32[1,8,32]{2,1,0:T(8,128)S(1)} %all_gather_reshape.10), channel_id=1, replica_groups=mesh['kvp'=16,'tp'=2] {'kvp'}, dimensions={0}, use_global_device_ids=true | all-gather | bytes 17408 | tf_op jit(solution)/shard_map/all_gather | solution.py:11
  69.8 36.0 %all_gather.9 = f32[16,8,32]{2,1,0:T(8,128)S(1)} all-gather(f32[1,8,32]{2,1,0:T(8,128)S(1)} %all_gather_reshape.9), channel_id=1, replica_groups=mesh['kvp'=16,'tp'=2] {'kvp'}, dimensions={0}, use_global_device_ids=true | all-gather | bytes 17408 | tf_op jit(solution)/shard_map/all_gather | solution.py:11
  105.9 0.0 all-gather.2.cloned.1.call-done
  105.9 0.9 slice_bitcast_fusion
  106.8 16.8 %while.19 = (s32[]{:T(128)}, f32[8,32]{1,0:T(8,128)S(1)}, f32[8,32]{1,0:T(8,128)S(1)}, f32[8,32,128]{2,1,0:T(8,128)S(1)}, f32[16,8,32]{2,1,0:T(8,128)S(1)}, /*in...) while((s32[]{:T(128)}, f32[8,32]{1,0:T(8,128)S(1)}, ...), condition=%wide.region_3.4_spmd, body=%wide.region_2.3_spmd.sunk | while | flops 99845 | bytes 403607 | solution.py:16
  106.8 1.1 fusion.44
  107.9 1.1 fusion.44
  109.1 1.1 fusion.44
  110.2 1.1 fusion.44
  111.3 1.1 fusion.44
  112.4 1.1 fusion.44
  113.5 1.1 fusion.44
  114.6 1.1 fusion.44
  115.8 1.1 fusion.44
  116.9 1.1 fusion.44
  118.0 1.1 fusion.44
  119.1 1.1 fusion.44
  120.2 1.1 fusion.44
  121.4 1.1 fusion.44
  122.5 1.1 fusion.44
  123.6 0.1 fusion.28
  123.7 0.0 copy-start.2
  123.7 0.0 copy-start.3
  123.7 2.9 fusion.35
  126.6 0.0 copy-done.2
  126.6 3.4 %psum.35 = f32[8,512]{1,0:T(8,128)S(1)} all-reduce(f32[8,512]{1,0:T(8,128)S(1)} %fusion.35), channel_id=1, replica_groups=mesh['kvp'=16,'tp'=2] {'tp'}, use_global_device_ids=true, to_apply=%region_4.5 | all-reduce | flops 4096 | bytes 32768 | tf_op jit(solution)/shard_map/psum | solution.py:74
  130.0 0.0 copy-done.3
  130.0 0.1 multiply_reduce_fusion
  130.1 38.6 %psum.36 = f32[8]{0:T(128)S(1)} all-reduce(f32[8]{0:T(128)S(1)} %get-tuple-element.201), channel_id=1, replica_groups=mesh['kvp'=16,'tp'=2] {'kvp'}, use_global_device_ids=true, to_apply=%region_6.7 | all-reduce | flops 8 | bytes 64 | tf_op jit(solution)/shard_map/psum | solution.py:75
  168.7 8.0 %fusion.32 = f32[8,14336]{1,0:T(8,128)} fusion(bf16[512,14336]{1,0:T(8,128)(2,1)} %param.21, f32[8,512]{1,0:T(8,128)S(1)} %get-tuple-element.202, f32[512]{0:T(512)S(1)} %convert_element_type.17, f32[8]{0:T(128)S(1)} %add_rsqrt_fusion), kind=kOutput, calls=%fused_computation.44 | convolution fusion | flops 117452800 | bytes 15157280 | tf_op jit(solution)/shard_map/dot_general | solution.py:78
  176.8 8.0 %fusion.31 = f32[8,14336]{1,0:T(8,128)} fusion(bf16[512,14336]{1,0:T(8,128)(2,1)} %param.22, f32[8,512]{1,0:T(8,128)S(1)} %get-tuple-element.202, f32[512]{0:T(512)S(1)} %convert_element_type.17, f32[8]{0:T(128)S(1)} %add_rsqrt_fusion), kind=kOutput, calls=%fused_computation.43 | convolution fusion | flops 117452800 | bytes 15157280 | tf_op jit(solution)/shard_map/dot_general | solution.py:79
  184.7 0.0 all-reduce.3.cloned.1.call-update
  184.8 107.5 %all-reduce.3.cloned.1.call-done = (f32[8,14336]{1,0:T(8,128)}, f32[8,14336]{1,0:T(8,128)}) async-done(((f32[8,14336]{1,0:T(8,128)}, f32[8,14336]{1,0:T(8,128)}), (f32[8,14336]{1,0:T(8,128)}, f32[8,14336]{1,0:T(8,128)})) %all-reduce.3.cloned.1.call-update) | async-done | bytes 917520 | tf_op jit(solution)/shard_map/psum | solution.py:80
  292.3 7.5 %fusion.19 = f32[8,512]{1,0:T(8,128)S(1)} fusion(bf16[14336,512]{1,0:T(8,128)(2,1)} %param.23, f32[8,14336]{1,0:T(8,128)} %get-tuple-element.195, f32[8,14336]{1,0:T(8,128)} %get-tuple-element.196), kind=kOutput, calls=%fused_computation.20 | convolution fusion | flops 118128640 | bytes 15613952 | tf_op jit(solution)/shard_map/dot_general | solution.py:82
  299.8 3.4 %psum.39 = f32[8,512]{1,0:T(8,128)S(1)} all-reduce(f32[8,512]{1,0:T(8,128)S(1)} %fusion.19), channel_id=1, replica_groups=mesh['kvp'=16,'tp'=2] {'tp'}, use_global_device_ids=true, to_apply=%region_9.10 | all-reduce | flops 4096 | bytes 32768 | tf_op jit(solution)/shard_map/psum | solution.py:83
  303.1 0.6 add.110
  (23 shorter events, 0.3 us)
Async XLA Ops:
  7.2 2.1 copy-start
  7.2 98.7 %all-gather.2.cloned.1.call-start = ((), (), s32[]{:S(2)}) async-start(), calls=%async_computation | async-start | bytes 2228224 | tf_op jit(solution)/shard_map/all_gather | solution.py:11
  18.9 4.0 %copy-start.5 = (s32[8]{0:T(128)S(1)}, s32[8]{0:T(128)}, u32[]{:S(2)}) copy-start(s32[8]{0:T(128)} %param.17) | copy-start | bytes 100
  18.9 4.1 %copy-start.6 = (bf16[8,4096]{1,0:T(8,128)(2,1)S(1)}, bf16[8,4096]{1,0:T(8,128)(2,1)}, u32[]{:S(2)}) copy-start(bf16[8,4096]{1,0:T(8,128)(2,1)} %param.13) | copy-start | bytes 196612
  22.9 2.5 copy-start.1
  25.4 1.6 copy-start.4
  26.6 265.7 %all-reduce.3.cloned.1.call-start = ((), (), s32[]{:S(2)}) async-start(), calls=%async_computation.1 | async-start | bytes 1835008 | tf_op jit(solution)/shard_map/psum | solution.py:80
  123.7 2.9 copy-start.2
  123.7 6.2 %copy-start.3 = (f32[8,512]{1,0:T(8,128)S(1)}, f32[8,512]{1,0:T(8,128)}, u32[]{:S(2)}) copy-start(f32[8,512]{1,0:T(8,128)} %param.18) | copy-start | bytes 49156
Sparse Core Ops, SparseCore 0:
  26.7 63.5 all-gather.1
  184.9 107.3 all-reduce.2
where the time goes:
time: 311 us
  blocking collectives  124 us (40%)
  waiting for transfers between devices  108 us (35%)
  matrix products  29.9 us (10%)
  other arithmetic  18.9 us (6%)
  local copies, waits for them, and re-layouts  15.4 us (5%)
  between operations  14.1 us (5%)
    psum x1, waiting for transfers between devices, body(): gate_full, up_full = lax.psum((gate_part, up_part), 'kvp')  108 us
    all_gather x2, blocking collectives, merged(): gathered = jax.tree.map(lambda a: lax.all_gather(a, axis), part)  78.9 us
    psum x1, blocking collectives, body(): squares = lax.psum(jnp.sum(mixed * mixed, axis=1), 'kvp')  38.6 us
    add x15, other arithmetic, combine(): out_early * factor_early[..., None] + out_late * factor_late[..., None]  16.1 us
    dot_general x1, matrix products, body(): gate_part = jnp.dot(normed, gate_weight, preferred_element_type=jnp.float32)  8.02 us
    dot_general x1, matrix products, body(): up_part = jnp.dot(normed, up_weight, preferred_element_type=jnp.float32)  7.99 us
    dot_general x1, matrix products, body(): down_part = jnp.dot(hidden, down_weight, preferred_element_type=jnp.float32)  7.46 us
  transfers between devices with their start and end apart: 2, of which 1 were waited for; matrix products, arithmetic and copies ran while one was open for 0% of the time, Pallas kernels for 0%

commit v1 on v0

--- a/solution.py
+++ b/solution.py
@@ -2,6 +2,7 @@
 import jax.numpy as jnp
 from jax import lax
 from jax.sharding import PartitionSpec as P
+from jax.lax import all_gather
 
 D = 8192
 HD = 128
@@ -72,7 +73,8 @@
     )
     projected = jnp.dot(attended, out_weight, preferred_element_type=jnp.float32)
     mixed = residual_in + lax.psum(projected, "tp")
-    squares = lax.psum(jnp.sum(mixed * mixed, axis=1), "kvp")
+    local_block = jnp.sum(mixed * mixed, axis=1)
+    squares = jnp.sum(all_gather(local_block, "kvp"), axis=0)
     inv_rms = lax.rsqrt(squares / D + 0.1)
     normed = (mixed * inv_rms[:, None] * norm_gain.astype(jnp.float32)).astype(jnp.bfloat16)
     gate_part = jnp.dot(normed, gate_weight, preferred_element_type=jnp.float32)

time: 311 us -> 313 us (level)
    psum x1 -> x0, blocking collectives: 38.6 us -> none  [body(): squares = lax.psum(jnp.sum(mixed * mixed, axis=1), 'kvp')]
    unnamed x0 -> x1, blocking collectives: none -> 38.2 us
where the time goes in v1:
time: 313 us; the launch traced here: 312 us
  blocking collectives  124 us (40%)
  waiting for transfers between devices  108 us (35%)
  matrix products  29.9 us (10%)
  other arithmetic  18.9 us (6%)
  local copies, waits for them, and re-layouts  16.3 us (5%)
  between operations  14.8 us (5%)
    psum x1, waiting for transfers between devices, body(): gate_full, up_full = lax.psum((gate_part, up_part), 'kvp')  108 us
    all_gather x2, blocking collectives, merged(): gathered = jax.tree.map(lambda a: lax.all_gather(a, axis), part)  79.1 us
    unnamed x1, blocking collectives  38.2 us
    add x15, other arithmetic, combine(): out_early * factor_early[..., None] + out_late * factor_late[..., None]  16.1 us
    dot_general x1, matrix products, body(): gate_part = jnp.dot(normed, gate_weight, preferred_element_type=jnp.float32)  8.03 us
    dot_general x1, matrix products, body(): up_part = jnp.dot(normed, up_weight, preferred_element_type=jnp.float32)  7.99 us
    dot_general x1, matrix products, body(): down_part = jnp.dot(hidden, down_weight, preferred_element_type=jnp.float32)  7.46 us
  transfers between devices with their start and end apart: 2, of which 1 were waited for; matrix products, arithmetic and copies ran while one was open for 0% of the time, Pallas kernels for 0%

profile of v1, /device:TPU:0, one launch (start us, length us, event | category | flops | bytes accessed | tf_op | source)
XLA Modules:
  0.0 312.3 jit_solution(6411887890923350178)
XLA Ops:
  7.2 0.0 copy-start
  7.2 0.0 all-gather.3.cloned.1.call-start
  7.2 0.5 broadcast.84
  7.8 1.4 reduce.3
  9.1 0.1 reshape_squeeze.3
  9.2 0.1 reshape.87
  9.3 0.0 copy-done
  9.3 2.0 gather_fusion
  11.3 4.0 %reshape.81 = bf16[8,256,4,128]{3,2,1,0:T(4,128)(2,1)} reshape(bf16[32,64,512]{2,1,0:T(8,128)(2,1)} %gather_fusion) | data formatting | bytes 4194304 | tf_op jit(solution)/shard_map/reshape | solution.py:54
  15.3 3.6 %gather_fusion.1 = bf16[32,64,512]{2,1,0:T(8,128)(2,1)} fusion(bf16[32,64,512]{2,1,0:T(8,128)(2,1)} %param.15, s32[1024]{0:T(1024)S(1)} %pad_clamp_fusion), kind=kCustom, calls=%fused_computation.1 | custom fusion | bytes 4194432 | tf_op jit(solution)/shard_map/gather | solution.py:55
  18.9 0.0 copy-start.5
  18.9 4.0 %reshape.83 = bf16[8,256,4,128]{3,2,1,0:T(4,128)(2,1)} reshape(bf16[32,64,512]{2,1,0:T(8,128)(2,1)} %gather_fusion.1) | data formatting | bytes 4194304 | tf_op jit(solution)/shard_map/reshape | solution.py:55
  22.9 0.0 copy-done.5
  22.9 0.1 broadcast_compare_fusion
  22.9 0.0 copy-done.6
  23.0 2.5 fusion.34
  25.4 0.0 copy-start.7
  25.4 0.0 copy-done.1
  25.4 1.1 fusion.16
  26.5 0.0 all-gather.3.cloned.1.call-update
  26.6 0.0 all-reduce.4.cloned.1.call-start
  26.6 0.1 all_gather_reshape.9
  26.7 0.2 fusion.22
  26.9 0.1 all_gather_reshape.10
  27.0 0.0 copy-done.4
  27.0 0.0 copy-done.7
  27.0 0.6 dynamic-slice
  28.3 42.8 %all_gather.16 = f32[16,8,32]{2,1,0:T(8,128)S(1)} all-gather(f32[1,8,32]{2,1,0:T(8,128)S(1)} %all_gather_reshape.10), channel_id=1, replica_groups=mesh['kvp'=16,'tp'=2] {'kvp'}, dimensions={0}, use_global_device_ids=true | all-gather | bytes 17408 | tf_op jit(solution)/shard_map/all_gather | solution.py:12
  71.1 36.3 %all_gather.15 = f32[16,8,32]{2,1,0:T(8,128)S(1)} all-gather(f32[1,8,32]{2,1,0:T(8,128)S(1)} %all_gather_reshape.9), channel_id=1, replica_groups=mesh['kvp'=16,'tp'=2] {'kvp'}, dimensions={0}, use_global_device_ids=true | all-gather | bytes 17408 | tf_op jit(solution)/shard_map/all_gather | solution.py:12
  107.4 0.9 slice_bitcast_fusion
  108.3 16.8 %while.19 = (s32[]{:T(128)}, f32[8,32]{1,0:T(8,128)S(1)}, f32[8,32]{1,0:T(8,128)S(1)}, f32[8,32,128]{2,1,0:T(8,128)S(1)}, f32[16,8,32]{2,1,0:T(8,128)S(1)}, /*in...) while((s32[]{:T(128)}, f32[8,32]{1,0:T(8,128)S(1)}, ...), condition=%wide.region_3.4_spmd, body=%wide.region_2.3_spmd.sunk | while | flops 99845 | bytes 403607 | solution.py:17
  108.4 1.1 fusion.44
  109.5 1.1 fusion.44
  110.6 1.1 fusion.44
  111.7 1.1 fusion.44
  112.8 1.1 fusion.44
  114.0 1.1 fusion.44
  115.1 1.1 fusion.44
  116.2 1.1 fusion.44
  117.3 1.1 fusion.44
  118.4 1.1 fusion.44
  119.6 1.1 fusion.44
  120.7 1.1 fusion.44
  121.8 1.1 fusion.44
  122.9 1.1 fusion.44
  124.0 1.1 fusion.44
  125.1 0.1 fusion.28
  125.3 0.0 copy-start.2
  125.3 0.0 copy-start.3
  125.3 2.9 fusion.35
  128.1 0.0 copy-done.2
  128.1 3.4 %psum.28 = f32[8,512]{1,0:T(8,128)S(1)} all-reduce(f32[8,512]{1,0:T(8,128)S(1)} %fusion.35), channel_id=1, replica_groups=mesh['kvp'=16,'tp'=2] {'tp'}, use_global_device_ids=true, to_apply=%region_4.5 | all-reduce | flops 4096 | bytes 32768 | tf_op jit(solution)/shard_map/psum | solution.py:75
  131.5 0.0 copy-done.3
  131.5 0.1 multiply_reduce_fusion
  131.6 0.2 dynamic-update-slice
  131.9 38.2 %all-reduce = f32[128]{0:T(128)S(1)} all-reduce(f32[128]{0:T(128)S(1)} %dynamic-update-slice), channel_id=2, replica_groups=mesh['kvp'=16,'tp'=2] {'kvp'}, use_global_device_ids=true, to_apply=%add | all-reduce | flops 128 | bytes 1024
  170.1 0.1 reshape.101
  170.2 8.0 %fusion.32 = f32[8,14336]{1,0:T(8,128)} fusion(bf16[512,14336]{1,0:T(8,128)(2,1)} %param.21, f32[8,512]{1,0:T(8,128)S(1)} %get-tuple-element.202, f32[512]{0:T(512)S(1)} %convert_element_type.17, f32[8]{0:T(128)S(1)} %add_rsqrt_fusion), kind=kOutput, calls=%fused_computation.44 | convolution fusion | flops 117452800 | bytes 15157280 | tf_op jit(solution)/shard_map/dot_general | solution.py:80
  178.2 8.0 %fusion.31 = f32[8,14336]{1,0:T(8,128)} fusion(bf16[512,14336]{1,0:T(8,128)(2,1)} %param.22, f32[8,512]{1,0:T(8,128)S(1)} %get-tuple-element.202, f32[512]{0:T(512)S(1)} %convert_element_type.17, f32[8]{0:T(128)S(1)} %add_rsqrt_fusion), kind=kOutput, calls=%fused_computation.43 | convolution fusion | flops 117452800 | bytes 15157280 | tf_op jit(solution)/shard_map/dot_general | solution.py:81
  186.2 0.0 all-reduce.4.cloned.1.call-update
  186.3 107.8 %all-reduce.4.cloned.1.call-done = (f32[8,14336]{1,0:T(8,128)}, f32[8,14336]{1,0:T(8,128)}) async-done(((f32[8,14336]{1,0:T(8,128)}, f32[8,14336]{1,0:T(8,128)}), (f32[8,14336]{1,0:T(8,128)}, f32[8,14336]{1,0:T(8,128)})) %all-reduce.4.cloned.1.call-update) | async-done | bytes 917520 | tf_op jit(solution)/shard_map/psum | solution.py:82
  294.0 7.5 %fusion.19 = f32[8,512]{1,0:T(8,128)S(1)} fusion(bf16[14336,512]{1,0:T(8,128)(2,1)} %param.23, f32[8,14336]{1,0:T(8,128)} %get-tuple-element.195, f32[8,14336]{1,0:T(8,128)} %get-tuple-element.196), kind=kOutput, calls=%fused_computation.20 | convolution fusion | flops 118128640 | bytes 15613952 | tf_op jit(solution)/shard_map/dot_general | solution.py:84
  301.5 3.4 %psum.31 = f32[8,512]{1,0:T(8,128)S(1)} all-reduce(f32[8,512]{1,0:T(8,128)S(1)} %fusion.19), channel_id=1, replica_groups=mesh['kvp'=16,'tp'=2] {'tp'}, use_global_device_ids=true, to_apply=%region_9.10 | all-reduce | flops 4096 | bytes 32768 | tf_op jit(solution)/shard_map/psum | solution.py:85
  304.9 0.6 add.112
  (29 shorter events, 0.3 us)
Async XLA Ops:
  7.2 2.1 copy-start
  7.2 100.2 %all-gather.3.cloned.1.call-start = ((), (), s32[]{:S(2)}) async-start(), calls=%async_computation | async-start | bytes 2228224 | tf_op jit(solution)/shard_map/all_gather | solution.py:12
  18.9 4.0 %copy-start.5 = (s32[8]{0:T(128)S(1)}, s32[8]{0:T(128)}, u32[]{:S(2)}) copy-start(s32[8]{0:T(128)} %param.17) | copy-start | bytes 100
  18.9 4.1 %copy-start.6 = (bf16[8,4096]{1,0:T(8,128)(2,1)S(1)}, bf16[8,4096]{1,0:T(8,128)(2,1)}, u32[]{:S(2)}) copy-start(bf16[8,4096]{1,0:T(8,128)(2,1)} %param.13) | copy-start | bytes 196612
  22.9 2.6 copy-start.1
  25.4 1.6 copy-start.4
  25.4 1.6 copy-start.7
  26.6 267.5 %all-reduce.4.cloned.1.call-start = ((), (), s32[]{:S(2)}) async-start(), calls=%async_computation.1 | async-start | bytes 1835008 | tf_op jit(solution)/shard_map/psum | solution.py:82
  125.3 2.9 copy-start.2
  125.3 6.2 %copy-start.3 = (f32[8,512]{1,0:T(8,128)S(1)}, f32[8,512]{1,0:T(8,128)}, u32[]{:S(2)}) copy-start(f32[8,512]{1,0:T(8,128)} %param.18) | copy-start | bytes 49156
Sparse Core Ops, SparseCore 0:
  26.7 63.3 all-gather.2
  186.4 107.6 all-reduce.3
